TPU v7x, 32 devices: a whole 2x2x4 slice. The times are simulated.
32 devices in a mesh: seq: 8 (over z, y), head: 4 (over x, core).
Axes of the slice: x: 2, y: 2, z: 4, core: 2. Of those that a mesh axis runs over, the one named last changes fastest.
Arguments:
- hidden_states: bfloat16 [2048, 1536], P('seq', 'head'), may hold values from -60 to 60
- feature_q: bfloat16 [1536, 384], P(None, 'head'), may hold values from -0.15625 to 0.15625
- feature_k: bfloat16 [1536, 384], P(None, 'head'), may hold values from -0.15625 to 0.15625
- value_w: bfloat16 [1536, 1536], P(None, 'head'), may hold values from -0.15625 to 0.15625
- window_q: bfloat16 [1536, 1536], P(None, 'head'), may hold values from -0.15625 to 0.15625
- window_k: bfloat16 [1536, 1536], P(None, 'head'), may hold values from -0.15625 to 0.15625
- norm_gain: float32 [1536], P('head'), may hold values from 0.5 to 1.5
Outputs:
- mixed: bfloat16 [2048, 1536], P('seq', 'head')
All inputs are finite; a program needn't handle non-finite values.
Results may differ from a plain program's by a relative error of at most 0.007.
Values may be sent and summed in bfloat16 or wider, within the bound.
A program may use at most 128 MiB of HBM per device.

v0:
```python
import jax
import jax.numpy as jnp
import numpy as np
from jax import lax
from jax.sharding import PartitionSpec as P

FK = 16
HV = 64
WINDOW_HEAD_SIZE = 64
WIN = 64


HIGH_ACCURACY = lax.Precision.HIGHEST


def from_behind(shard, axis, by):
    devices = lax.axis_size(axis)
    pairs = [(i, i + by) for i in range(devices) if 0 <= i + by < devices]
    return lax.ppermute(shard, axis, pairs)


def prefix_2(value, axis, join, neutral):
    count, mine = (lax.axis_size(axis), lax.axis_index(axis))
    pieces = lax.all_gather(value, axis)
    so_far = jnp.full_like(value, 0) + jnp.asarray(neutral, value.dtype)

    def lap(position, so_far):
        longer = join(so_far, pieces[position])
        return jnp.where(position < mine, longer, so_far)

    return lax.fori_loop(0, count - 1, lap, so_far)


def expand(x):
    lead = x.shape[:-1]
    width = x.shape[-1]
    ones = jnp.ones(lead + (1,), jnp.float32)
    upper, lower = np.triu_indices(width)
    weight = np.where(upper == lower, 0.5**0.5, 1.0).astype(np.float32)
    quad = x[..., upper] * x[..., lower] * weight
    return jnp.concatenate([ones, x, quad], axis=-1)


def add_states(earlier, later):
    return earlier + later


def body(hidden_states, feature_q, feature_k, value_w, window_q, window_k, norm_gain):
    rows = hidden_states.shape[0]
    heads = feature_q.shape[1] // FK
    offset = lax.axis_index("seq") * rows
    whole = lax.all_gather(hidden_states, "head", axis=1, tiled=True)
    query = (jnp.dot(whole, feature_q, preferred_element_type=jnp.float32) * FK ** (-0.25)).reshape(
        rows, heads, FK
    )
    key = (jnp.dot(whole, feature_k, preferred_element_type=jnp.float32) * FK ** (-0.25)).reshape(
        rows, heads, FK
    )
    wquery = jnp.dot(whole, window_q, preferred_element_type=jnp.float32).astype(jnp.bfloat16)
    wkey = jnp.dot(whole, window_k, preferred_element_type=jnp.float32).astype(jnp.bfloat16)
    values_ext = jnp.dot(whole, value_w, preferred_element_type=jnp.float32).astype(jnp.bfloat16)
    prev_keys, prev_values = from_behind((wkey[rows - WIN :], values_ext[rows - WIN :]), "seq", 1)
    key_rows_full = jnp.concatenate([prev_keys, wkey], axis=0)
    values_all = jnp.concatenate([prev_values, values_ext], axis=0)
    value3 = values_ext.reshape(rows, heads, HV)
    phi_q = expand(query)
    phi_k = expand(key)
    width = phi_k.shape[-1]
    local_state = jnp.einsum(
        "lhf,lhv->fhv", phi_k, value3.astype(jnp.float32), precision=HIGH_ACCURACY
    ).reshape(width, heads * HV)
    prefix = prefix_2(local_state, "seq", add_states, jnp.zeros_like(local_state))
    inner = jnp.einsum("lhf,mhf->hlm", query, key, precision=HIGH_ACCURACY)
    kernel = 1.0 + inner + 0.5 * inner * inner
    index_rows = jnp.arange(rows, dtype=jnp.int32)
    causal = index_rows[:, None] >= index_rows[None, :]
    kernel = jnp.where(causal[None], kernel, 0.0).astype(jnp.bfloat16)
    intra = jnp.einsum("hlm,mhv->lhv", kernel, value3, preferred_element_type=jnp.float32)
    cross = jnp.einsum(
        "lhf,fhv->lhv", phi_q, prefix.reshape(width, heads, HV), precision=HIGH_ACCURACY
    )
    linear = intra + cross
    scale = lax.rsqrt(jnp.mean(linear * linear, axis=-1, keepdims=True) + 1e-05)
    normed = linear * scale * norm_gain.reshape(heads, HV)
    query_weight3 = wquery.reshape(rows, heads, WINDOW_HEAD_SIZE)
    key_tensor3 = key_rows_full.reshape(rows + WIN, heads, WINDOW_HEAD_SIZE)
    window_logits = jnp.einsum(
        "qxo,bxo->xqb", query_weight3, key_tensor3, preferred_element_type=jnp.float32
    ) * WINDOW_HEAD_SIZE ** (-0.5)
    query_pos = offset + index_rows[:, None]
    key_pos = offset - WIN + jnp.arange(rows + WIN, dtype=jnp.int32)[None, :]
    valid = (key_pos <= query_pos) & (key_pos > query_pos - WIN) & (key_pos >= 0)
    window_logits = jnp.where(valid[None], window_logits, -1e30)
    top = jnp.max(window_logits, axis=-1, keepdims=True)
    expw = jnp.exp(window_logits - top)
    weights = (expw / jnp.sum(expw, axis=-1, keepdims=True)).astype(jnp.bfloat16)
    window = jnp.einsum(
        "hlm,mhv->lhv",
        weights,
        values_all.reshape(rows + WIN, heads, HV),
        preferred_element_type=jnp.float32,
    )
    return (normed + window).astype(jnp.bfloat16).reshape(rows, heads * HV)


def solution(mesh):
    in_specs = (
        P("seq", "head"),
        P(None, "head"),
        P(None, "head"),
        P(None, "head"),
        P(None, "head"),
        P(None, "head"),
        P("head"),
    )
    out_specs = P("seq", "head")
    return jax.shard_map(body, mesh=mesh, in_specs=in_specs, out_specs=out_specs, check_vma=False)
```

profile of v0, /device:TPU:0, one launch (start us, length us, event | category | flops | bytes accessed | tf_op | source)
XLA Modules:
  0.0 101.9 jit_solution(2306110077940659043)
XLA Ops:
  6.5 10.4 %all_gather.6 = bf16[256,1536]{1,0:T(8,128)(2,1)S(1)} all-gather(bf16[256,384]{1,0:T(8,128)(2,1)} %param.19), channel_id=1, replica_groups=mesh['seq'=8,'head'=4] {'head'}, dimensions={1}, use_global_device_ids=true | all-gather | bytes 983040 | tf_op jit(solution)/shard_map/all_gather | solution.py:52
  17.0 1.5 %convolution_multiply_fusion = f32[256,96]{0,1:T(8,128)S(1)} fusion(bf16[256,1536]{1,0:T(8,128)(2,1)S(1)} %all_gather.6, bf16[1536,96]{0,1:T(8,128)(2,1)} %param.21), kind=kOutput, calls=%fused_computation.22 | convolution fusion | flops 75522048 | bytes 1179648 | tf_op jit(solution)/shard_map/dot_general | solution.py:56
  20.7 1.6 %convolution_multiply_fusion.1 = f32[256,96]{0,1:T(8,128)S(1)} fusion(bf16[256,1536]{1,0:T(8,128)(2,1)} %copy-done.1, bf16[1536,96]{0,1:T(8,128)(2,1)} %param.20), kind=kOutput, calls=%fused_computation.23 | convolution fusion | flops 75522048 | bytes 1179648 | tf_op jit(solution)/shard_map/dot_general | solution.py:53
  23.0 1.8 %gather_fusion.2 = f32[136,256,6]{1,2,0:T(8,128)} fusion(f32[256,6,16]{0,1,2:T(8,128)S(1)} %copy.48, s32[1024]{0:T(1024)S(1)} %pad_clamp_fusion.1), kind=kCustom, calls=%fused_computation.2 | custom fusion | bytes 1671712 | tf_op jit(solution)/shard_map/gather | solution.py:40
  24.8 1.8 %gather_fusion.3 = f32[136,256,6]{1,2,0:T(8,128)} fusion(f32[256,6,16]{0,1,2:T(8,128)S(1)} %copy.48, s32[1024]{0:T(1024)S(1)} %pad_clamp_fusion), kind=kCustom, calls=%fused_computation.3 | custom fusion | bytes 1671712 | tf_op jit(solution)/shard_map/gather | solution.py:40
  26.6 2.4 %convolution_convert_fusion.2 = bf16[256,384]{1,0:T(8,128)(2,1)} fusion(bf16[256,1536]{1,0:T(8,128)(2,1)} %copy-done.1, bf16[1536,384]{1,0:T(8,128)(2,1)S(1)} %copy-done), kind=kOutput, calls=%fused_computation.20 | convolution fusion | flops 302088192 | bytes 2162688 | tf_op jit(solution)/shard_map/dot_general | solution.py:61
  29.0 1.8 %copy.41 = bf16[256,384]{0,1:T(8,128)(2,1)} copy(bf16[256,384]{1,0:T(8,128)(2,1)} %convolution_convert_fusion.2) | data formatting | bytes 393216 | tf_op jit(solution)/shard_map/convert_element_type | solution.py:61
  30.8 3.5 %fusion.21 = (f32[256,6,136]{0,2,1:T(8,128)}, f32[256,6,136]{0,2,1:T(8,128)S(1)}) fusion(f32[136,256,6]{1,2,0:T(8,128)} %gather_fusion.3, f32[136,256,6]{1,2,0:T(8,128)} %gather_fusion.2, f32[136]{0:T(256)S(1)} %copy-done.14, f32[136,256,6]{1,2,0:T(8,128)S(1)} %gather_fusion.1, f32[136,256,6]{1,2,0:T(8,128)S(1)} %gather_fusion), kind=kLoop, calls=%fused_computation.38 | loop fusion | flops 835584 | bytes 5014048 | tf_op jit(solution)/shard_map/mul | solution.py:40
  35.1 0.8 copy.46
  35.9 1.8 %convolution_convert_fusion = bf16[256,384]{1,0:T(8,128)(2,1)S(1)} fusion(bf16[256,1536]{1,0:T(8,128)(2,1)S(1)} %copy-done.2, bf16[1536,384]{1,0:T(8,128)(2,1)} %param.24), kind=kOutput, calls=%fused_computation.18 | convolution fusion | flops 302088192 | bytes 2162688 | tf_op jit(solution)/shard_map/dot_general | solution.py:60
  37.8 3.6 %collective-permute-start.1 = (bf16[64,384]{1,0:T(8,128)(2,1)S(1)}, bf16[64,384]{1,0:T(8,128)(2,1)S(1)}, u32[]{:S(2)}, u32[]{:S(2)}) collective-permute-start(bf16[64,384]{1,0:T(8,128)(2,1)S(1)} %slice.17), channel_id=1, source_target_pairs={{0,4},{4,8},{8,12},{12,16},{16,20},{20,24},{24,28},{1,5},{5,9},{9,... | collective-permute-start | bytes 147464 | tf_op jit(solution)/shard_map/ppermute | solution.py:19
  41.4 4.0 %collective-permute-start = (bf16[64,384]{1,0:T(8,128)(2,1)S(1)}, bf16[64,384]{1,0:T(8,128)(2,1)}, u32[]{:S(2)}, u32[]{:S(2)}) collective-permute-start(bf16[64,384]{1,0:T(8,128)(2,1)S(1)} %slice.16), channel_id=1, source_target_pairs={{0,4},{4,8},{8,12},{12,16},{16,20},{20,24},{24,28},{1,5},{5,9},{9,... | collective-permute-start | bytes 147464 | tf_op jit(solution)/shard_map/ppermute | solution.py:19
  45.5 1.7 %fusion.4 = bf16[6,256,256]{2,1,0:T(8,128)(2,1)S(1)} fusion(f32[256,6,16]{0,2,1:T(8,128)S(1)} %bitcast.52, f32[256,6,16]{0,2,1:T(8,128)S(1)} %bitcast.56, pred[256,256]{1,0:T(8,128)(4,1)S(1)} %iota_compare_fusion), kind=kOutput, calls=%fused_computation.13 | convolution fusion | flops 77856768 | bytes 1048576 | tf_op jit(solution)/shard_map/lhf,mhf->hlm/dot_general | solution.py:73
  49.9 2.1 %fusion.32 = (f32[6,256]{1,0:T(8,128)S(1)}, f32[6,256,320]{1,2,0:T(8,128)}) fusion(pred[256,320]{0,1:T(8,128)(4,1)S(1)} %and_and_fusion, bf16[256,6,64]{0,2,1:T(8,128)(2,1)S(1)} %bitcast.59, bf16[320,6,64]{0,2,1:T(8,128)(2,1)S(1)} %bitcast.58), kind=kOutput, calls=%fused_computation.61 | convolution fusion | flops 64880960 | bytes 2496512 | tf_op jit(solution)/shard_map/sub | solution.py:95
  51.9 32.9 %all-gather.2.cloned.1.call-done = f32[8,153,384]{2,1,0:T(8,128)} async-done(((f32[1,153,384]{2,1,0:T(8,128)}), f32[8,153,384]{2,1,0:T(8,128)}) %all-gather.2.cloned.1.call-update) | async-done | bytes 1880080 | tf_op jit(solution)/shard_map/all_gather | solution.py:24
  84.8 7.3 %while.14 = (s32[]{:T(128)}, f32[153,384]{1,0:T(8,128)S(1)}, s32[]{:T(128)}, f32[8,153,384]{2,1,0:T(8,128)}, s32[]{:T(128)}, /*index=5*/s32[]{:T(128)}) while((s32[]{:T(128)}, f32[153,384]{1,0:T(8,128)S(1)}, s32[]{:T(128)}, f32[8,153,384]{2,1,0:T(8,128)}, s32[]{:T(128)}, /*index=5*/s32[]{:T(128)}) %tuple.36), condition=%wide.region_1.2_spmd.clone, body=%wide.region_0.1_spmd.clone.sunk | while | flops 176260 | bytes 705117 | solution.py:31
  84.8 1.1 %add_select_fusion.2 = f32[153,384]{1,0:T(8,128)S(1)} fusion(f32[153,384]{1,0:T(8,128)S(1)} %get-tuple-element.148, f32[8,153,384]{2,1,0:T(8,128)} %get-tuple-element.156, s32[]{:T(128)} %get-tuple-element.147, pred[]{:T(512)S(6)} %compare.3, pred[]{:T(512)S(6)} %lt.21), kind=kLoop, calls=%fused_computation.4.clone.1 | loop fusion | flops 176256 | bytes 705030 | tf_op jit(solution)/shard_map/while/body/eval_jaxpr/jit(_where)/select_n | solution.py:29
  85.9 1.0 add_select_fusion.2
  87.0 1.0 add_select_fusion.2
  88.0 1.0 add_select_fusion.2
  89.1 1.0 add_select_fusion.2
  90.1 1.0 add_select_fusion.2
  91.1 1.0 add_select_fusion.2
  92.4 0.8 multiply_reduce_fusion
  (70 shorter events, 8.4 us)
Async XLA Ops:
  6.5 20.0 %copy-start = (bf16[1536,384]{1,0:T(8,128)(2,1)S(1)}, bf16[1536,384]{1,0:T(8,128)(2,1)}, u32[]{:S(2)}) copy-start(bf16[1536,384]{1,0:T(8,128)(2,1)} %param.22) | copy-start | bytes 3538948
  6.5 12.0 %copy-start.15 = (s32[136]{0:T(256)S(1)}, s32[136]{0:T(256)}, u32[]{:S(2)}) copy-start(s32[136]{0:T(256)} %constant.74) | copy-start | bytes 1636
  6.5 12.6 %copy-start.16 = (s32[136]{0:T(256)S(1)}, s32[136]{0:T(256)}, u32[]{:S(2)}) copy-start(s32[136]{0:T(256)} %constant.75) | copy-start | bytes 1636
  6.5 78.3 %all-gather.2.cloned.1.call-start = ((), (), s32[]{:S(2)}) async-start(), calls=%async_computation | async-start | bytes 2211840 | tf_op jit(solution)/shard_map/all_gather | solution.py:24
  17.0 1.6 %copy-start.1 = (bf16[256,1536]{1,0:T(8,128)(2,1)}, bf16[256,1536]{1,0:T(8,128)(2,1)S(1)}, u32[]{:S(2)}) copy-start(bf16[256,1536]{1,0:T(8,128)(2,1)S(1)} %all_gather.6) | copy-start | bytes 2359300
  18.5 0.6 copy-start.9
  22.3 0.6 copy-start.7
  26.6 4.2 %copy-start.14 = (f32[136]{0:T(256)S(1)}, f32[136]{0:T(256)}, u32[]{:S(2)}) copy-start(f32[136]{0:T(256)} %constant.71.clone) | copy-start | bytes 1636
  30.7 3.5 %copy-start.11 = (f32[153]{0:T(256)}, f32[153]{0:T(256)S(1)}, u32[]{:S(2)}) copy-start(f32[153]{0:T(256)S(1)} %pad.7.clone) | copy-start | bytes 1840
  30.7 3.5 %copy-start.4 = (bf16[256,384]{0,1:T(8,128)(2,1)S(1)}, bf16[256,384]{0,1:T(8,128)(2,1)}, u32[]{:S(2)}) copy-start(bf16[256,384]{0,1:T(8,128)(2,1)} %copy.41) | copy-start | bytes 589828
  30.7 3.5 %copy-start.10 = (f32[256,96]{0,1:T(8,128)S(1)}, f32[256,96]{0,1:T(8,128)}, u32[]{:S(2)}) copy-start(f32[256,96]{0,1:T(8,128)} %copy-done.9) | copy-start | bytes 294916
  34.2 1.7 %copy-start.2 = (bf16[256,1536]{1,0:T(8,128)(2,1)S(1)}, bf16[256,1536]{1,0:T(8,128)(2,1)}, u32[]{:S(2)}) copy-start(bf16[256,1536]{1,0:T(8,128)(2,1)} %copy-done.1) | copy-start | bytes 2359300
  35.0 6.3 %copy-start.6 = (bf16[256,384]{1,0:T(8,128)(2,1)S(1)}, bf16[256,384]{1,0:T(8,128)(2,1)}, u32[]{:S(2)}) copy-start(bf16[256,384]{1,0:T(8,128)(2,1)} %convolution_convert_fusion.2) | copy-start | bytes 589828
  35.1 10.4 %copy-start.8 = (f32[256,96]{0,1:T(8,128)S(1)}, f32[256,96]{0,1:T(8,128)}, u32[]{:S(2)}) copy-start(f32[256,96]{0,1:T(8,128)} %copy-done.7) | copy-start | bytes 294916
  37.8 9.4 %copy-start.5 = (bf16[256,384]{0,1:T(8,128)(2,1)S(1)}, bf16[256,384]{0,1:T(8,128)(2,1)}, u32[]{:S(2)}) copy-start(bf16[256,384]{0,1:T(8,128)(2,1)} %copy.41) | copy-start | bytes 589828
  37.8 10.7 %collective-permute-start.1 = (bf16[64,384]{1,0:T(8,128)(2,1)S(1)}, bf16[64,384]{1,0:T(8,128)(2,1)S(1)}, u32[]{:S(2)}, u32[]{:S(2)}) collective-permute-start(bf16[64,384]{1,0:T(8,128)(2,1)S(1)} %slice.17), channel_id=1, source_target_pairs={{0,4},{4,8},{8,12},{12,16},{16,20},{20,24},{24,28},{1,5},{5,9},{9,... | collective-permute-start | bytes 147464 | tf_op jit(solution)/shard_map/ppermute | solution.py:19
  41.4 7.4 %collective-permute-start = (bf16[64,384]{1,0:T(8,128)(2,1)S(1)}, bf16[64,384]{1,0:T(8,128)(2,1)}, u32[]{:S(2)}, u32[]{:S(2)}) collective-permute-start(bf16[64,384]{1,0:T(8,128)(2,1)S(1)} %slice.16), channel_id=1, source_target_pairs={{0,4},{4,8},{8,12},{12,16},{16,20},{20,24},{24,28},{1,5},{5,9},{9,... | collective-permute-start | bytes 147464 | tf_op jit(solution)/shard_map/ppermute | solution.py:19
  45.5 2.1 %copy-start.17 = (bf16[1536,384]{1,0:T(8,128)(2,1)S(1)}, bf16[1536,384]{1,0:T(8,128)(2,1)}, u32[]{:S(2)}) copy-start(bf16[1536,384]{1,0:T(8,128)(2,1)} %param.23) | copy-start | bytes 3538948
  47.6 0.9 copy-start.13
  84.8 7.5 %copy-start.3 = (f32[256,6,136]{0,2,1:T(8,128)S(1)}, f32[256,6,136]{0,2,1:T(8,128)}, u32[]{:S(2)}) copy-start(f32[256,6,136]{0,2,1:T(8,128)} %get-tuple-element.108) | copy-start | bytes 2506756
  84.8 7.5 %copy-start.12 = (f32[153]{0:T(256)S(1)}, f32[153]{0:T(256)}, u32[]{:S(2)}) copy-start(f32[153]{0:T(256)} %copy-done.11) | copy-start | bytes 1840
  92.3 1.5 %copy-start.18 = (f32[6,256,320]{1,2,0:T(8,128)S(1)}, f32[6,256,320]{1,2,0:T(8,128)}, u32[]{:S(2)}) copy-start(f32[6,256,320]{1,2,0:T(8,128)} %get-tuple-element.111) | copy-start | bytes 5898244
Sparse Core Ops, SparseCore 0:
  36.1 48.7 all-gather.1
where the time goes:
time: 102 us
  waiting for transfers between devices  32.9 us (32%)
  matrix products  14 us (14%)
  between operations  13.8 us (14%)
  other arithmetic  11.7 us (11%)
  local copies, waits for them, and re-layouts  11.4 us (11%)
  blocking collectives  10.4 us (10%)
  starting transfers between devices  7.6 us (7%)
    all_gather x1, waiting for transfers between devices, prefix_2(): pieces = lax.all_gather(value, axis)  32.9 us
    all_gather x1, blocking collectives, body(): whole = lax.all_gather(hidden_states, 'head', axis=1, tiled=True)  10.4 us
    ppermute x2, starting transfers between devices, from_behind(): return lax.ppermute(shard, axis, pairs)  7.6 us
    select_n x7, other arithmetic, lap(): return jnp.where(position < mine, longer, so_far)  7.18 us
    gather x4, local copies, waits for them, and re-layouts, expand(): quad = x[..., upper] * x[..., lower] * weight  5.12 us
    mul x1, other arithmetic, expand(): quad = x[..., upper] * x[..., lower] * weight  3.47 us
    dot_general x1, matrix products, body(): jnp.dot(whole, value_w, preferred_element_type=jnp.float32)  2.4 us
    sub x1, matrix products, body(): expw = jnp.exp(window_logits - top)  2.07 us
  transfers between devices with their start and end apart: 3, of which 1 were waited for; matrix products, arithmetic and copies ran while one was open for 8% of the time, Pallas kernels for 0%

commit v1 on v0

v1 whole, which is shorter than its diff:
```python
import functools

import jax
import jax.numpy as jnp
import numpy as np
from jax import lax
from jax.experimental import pallas as pl
from jax.experimental.pallas import tpu as pltpu
from jax.sharding import PartitionSpec as P

FK = 16
HV = 64
WIN = 64
LANES = 128
CHUNK = 256
MESH = pl.DeviceIdType.MESH
F32 = jnp.float32
BF16 = jnp.bfloat16


def features(heads):
    upper, lower = np.triu_indices(FK)
    one = heads * FK
    left, right, owner, weight = [], [], [], []
    for head in range(heads):
        base = head * FK
        left += [one] + [base + i for i in range(FK)] + [base + i for i in upper]
        right += [one] + [one] * FK + [base + j for j in lower]
        owner += [head] * (1 + FK + len(upper))
        weight += [1.0] * (1 + FK) + [0.5 if i == j else 1.0 for i, j in zip(upper, lower)]
    count = len(left)
    width = -(-count // CHUNK) * CHUNK
    ea = np.zeros((2 * LANES, width), np.float32)
    eb = np.zeros((2 * LANES, width), np.float32)
    mask = np.zeros((-(-heads // 8) * 8, width), np.float32)
    for lane in range(count):
        ea[[left[lane], LANES + left[lane]], lane] = 1.0
        eb[[right[lane], LANES + right[lane]], lane] = 1.0
        mask[owner[lane], lane] = weight[lane]
    return ea, eb, mask


def dot(a, b):
    return jnp.dot(a, b, preferred_element_type=F32)


def dot_t(a, b):
    return lax.dot_general(a, b, (((1,), (1,)), ((), ())), preferred_element_type=F32)


def split(x):
    high = x.astype(BF16)
    return high, (x - high.astype(F32)).astype(BF16)


def kernel(blocks, group, heads, wire, hid, fq, fk, vw, wqw, wkw, gain, ea, eb, mask, out,
           hbuf, fq_v, fk_v, vw_v, wq_v, wk_v, gain_v, ea_v, eb_v, mask_v,
           q_acc, k_acc, v_acc, wq_acc, wk_acc, v_b, wq_b, wk_b, halo_out, halo_in,
           phi_q, local, y_out, y_in, z_out, z_in, lin, win,
           load_sem, g_send, g_recv, h_send, h_recv, y_send, y_recv, z_send, z_recv):
    s, h = lax.axis_index("seq"), lax.axis_index("head")
    rows, depth = hid.shape
    chunks = local.shape[0]
    pair, inner = s // 2, s % 2
    last_pair = blocks // 2 - 1
    pairs = heads // 2

    loads = [
        pltpu.make_async_copy(src, dst, load_sem.at[i])
        for i, (src, dst) in enumerate((
            (hid, hbuf.at[h]), (fk, fk_v), (vw, vw_v), (wkw, wk_v), (fq, fq_v), (wqw, wq_v),
            (ea, ea_v), (eb, eb_v), (mask, mask_v), (gain, gain_v),
        ))
    ]
    for load in loads:
        load.start()

    barrier = pltpu.get_barrier_semaphore()
    bits = []
    bit = group // 2
    while bit:
        bits.append(bit)
        bit //= 2

    def flip(value, by):
        return value + by - 2 * by * ((value // by) % 2)

    for by in bits:
        pl.semaphore_signal(barrier, inc=1, device_id=(s, flip(h, by)), device_id_type=MESH)
    expected = len(bits)
    for by in (1, -1, 2, -2):
        there = s + by
        valid = jnp.logical_and(there >= 0, there < blocks)

        @pl.when(valid)
        def _(there=there):
            pl.semaphore_signal(barrier, inc=1, device_id=(there, h), device_id_type=MESH)

        expected = expected + jnp.where(valid, 1, 0)

    lane = lax.broadcasted_iota(jnp.int32, (rows, LANES), 1)
    fill = jnp.where(lane >= heads * FK, FK**0.25, 0.0).astype(F32)
    q_acc[...] = fill
    k_acc[...] = fill
    pl.semaphore_wait(barrier, expected)
    loads[0].wait()

    moves = {}

    def send_block(index, owner, by):
        move = pltpu.make_async_remote_copy(
            src_ref=hbuf.at[owner], dst_ref=hbuf.at[owner],
            send_sem=g_send.at[index], recv_sem=g_recv.at[index],
            device_id=(s, flip(h, by)), device_id_type=MESH,
        )
        move.start()
        return move

    plan = []

    def spread(owner_flip, from_level):
        for level in range(from_level, len(bits)):
            plan.append((owner_flip, level))
            spread(owner_flip ^ bits[level], level + 1)

    spread(0, 0)
    arrives = {}
    for index, (own, level) in enumerate(plan):
        arrives[own ^ bits[level]] = index

    def owner_of(mask_bits):
        value = h
        for by in bits:
            if mask_bits & by:
                value = flip(value, by)
        return value

    def forward(block):
        for index, (own, level) in enumerate(plan):
            if own == block:
                moves[index] = send_block(index, owner_of(block), bits[level])

    def arrive(block):
        moves_index = arrives[block]
        moves[moves_index].wait_recv()

    def part(weight, owner):
        return weight[pl.ds(pl.multiple_of(owner * depth, depth), depth), :]

    def part_t(weight, owner):
        return weight[:, pl.ds(pl.multiple_of(owner * depth, depth), depth)]

    forward(0)
    sequence = sorted(range(1, group), key=lambda b: (b.bit_length(), b))
    main = ((v_acc, vw_v), (wk_acc, wk_v), (wq_acc, wq_v))
    small = ((k_acc, fk_v), (q_acc, fq_v))
    for load in loads[1:6]:
        load.wait()
    for position, block in enumerate([0] + sequence):
        if block:
            arrive(block)
            forward(block)
        owner = owner_of(block)
        tile = hbuf[owner]
        final = position == group - 1
        for acc, weight in small:
            if final and acc is q_acc:
                continue
            acc[:, : heads * FK] += dot_t(tile, part_t(weight, owner))
        for acc, weight in main:
            if final and acc is wq_acc:
                continue
            product = dot(tile, part(weight, owner))
            acc[...] = product if position == 0 else acc[...] + product
    last_tile, last_owner = tile, owner

    v_b[...] = v_acc[...].astype(BF16)
    wk_b[...] = wk_acc[...].astype(BF16)
    width = heads * HV
    halo_out[:, :width] = wk_b[rows - WIN :, :]
    halo_out[:, width:] = v_b[rows - WIN :, :]
    after = lax.rem(s + 1, blocks)
    halo = pltpu.make_async_remote_copy(
        src_ref=halo_out, dst_ref=halo_in, send_sem=h_send, recv_sem=h_recv,
        device_id=(after, h), device_id_type=MESH,
    )

    @pl.when(s < blocks - 1)
    def _():
        halo.start()

    for load in loads[6:]:
        load.wait()

    k_high, k_low = split(k_acc[...] * FK**-0.25)
    k_cat = jnp.concatenate([k_high, k_low], axis=1)
    v_turned = v_b[...].T
    exchange = []
    for c in range(chunks):
        lanes = slice(c * CHUNK, (c + 1) * CHUNK)
        phi_k = (dot(k_cat, ea_v[:, lanes]) * dot(k_cat, eb_v[:, lanes])).astype(BF16)
        full = dot(v_turned, phi_k)
        state = full[:HV] * mask_v[0:1, lanes]
        for head in range(1, heads):
            state += full[head * HV : (head + 1) * HV] * mask_v[head : head + 1, lanes]
        local[c] = state
        y_out[c] = state.astype(wire)
        move = pltpu.make_async_remote_copy(
            src_ref=y_out.at[c], dst_ref=y_in.at[c], send_sem=y_send.at[c], recv_sem=y_recv.at[c],
            device_id=(flip(s, 1), h), device_id_type=MESH,
        )
        move.start()
        exchange.append(move)
    beyond = lax.rem(s + 2, blocks)
    chain = [
        pltpu.make_async_remote_copy(
            src_ref=z_out.at[c], dst_ref=z_in.at[c], send_sem=z_send.at[c], recv_sem=z_recv.at[c],
            device_id=(beyond, h), device_id_type=MESH,
        )
        for c in range(chunks)
    ]

    q_acc[:, : heads * FK] += dot_t(last_tile, part_t(fq_v, last_owner))
    wq_b[...] = (wq_acc[...] + dot(last_tile, part(wq_v, last_owner))).astype(BF16)
    q_high, q_low = split(q_acc[...] * FK**-0.25)
    q_cat = jnp.concatenate([q_high, q_low], axis=1)

    def features_q():
        for c in range(chunks):
            lanes = slice(c * CHUNK, (c + 1) * CHUNK)
            phi_q[:, lanes] = (dot(q_cat, ea_v[:, lanes]) * dot(q_cat, eb_v[:, lanes])).astype(BF16)

    k_twice = jnp.concatenate([k_high, k_high], axis=1)
    half = rows // 2
    lane_q = lax.broadcasted_iota(jnp.int32, (half, 2 * LANES), 1) % LANES // FK
    low_half = lax.broadcasted_iota(jnp.int32, (half, LANES), 1) < HV

    def intra(p, block):
        rs = slice(block * half, (block + 1) * half)
        keys = (block + 1) * half
        qs = q_cat[rs]
        stacked = jnp.concatenate(
            [jnp.where(lane_q == 2 * p, qs, 0), jnp.where(lane_q == 2 * p + 1, qs, 0)], axis=0
        )
        a = dot_t(stacked, k_twice[:keys]) + dot_t(stacked[:, :LANES], k_low[:keys])
        kern = 1.0 + a + 0.5 * a * a
        row = lax.broadcasted_iota(jnp.int32, a.shape, 0) % half + block * half
        col = lax.broadcasted_iota(jnp.int32, a.shape, 1)
        kern = jnp.where(row >= col, kern, 0.0).astype(BF16)
        both = dot(kern, v_b[:keys, p * LANES : (p + 1) * LANES])
        lin[rs, p * LANES : (p + 1) * LANES] = jnp.where(low_half, both[:half], both[half:])

    low_win = lax.broadcasted_iota(jnp.int32, (WIN, LANES), 1) < HV
    row_w = lax.broadcasted_iota(jnp.int32, (2 * WIN, 2 * WIN), 0) % WIN
    col_w = lax.broadcasted_iota(jnp.int32, (2 * WIN, 2 * WIN), 1)
    seen = jnp.logical_and(col_w > row_w, col_w <= row_w + WIN)

    def window(p, block):
        ls = slice(p * LANES, (p + 1) * LANES)
        qs = wq_b[block * WIN : (block + 1) * WIN, ls]
        stacked = jnp.concatenate([jnp.where(low_win, qs, 0), jnp.where(low_win, 0, qs)], axis=0)
        valid = seen
        if block == 0:
            keys = jnp.concatenate([halo_in[:, ls], wk_b[:WIN, ls]], axis=0)
            vals = jnp.concatenate(
                [halo_in[:, width + p * LANES : width + (p + 1) * LANES], v_b[:WIN, ls]], axis=0
            )
            valid = jnp.logical_and(seen, jnp.logical_or(col_w >= WIN, s > 0))
        else:
            keys = wk_b[(block - 1) * WIN : (block + 1) * WIN, ls]
            vals = v_b[(block - 1) * WIN : (block + 1) * WIN, ls]
        logits = jnp.where(valid, dot_t(stacked, keys) * HV**-0.5, -1e30)
        expw = jnp.exp(logits - jnp.max(logits, axis=-1, keepdims=True))
        weights = (expw / jnp.sum(expw, axis=-1, keepdims=True)).astype(BF16)
        both = dot(weights, vals)
        win[block * WIN : (block + 1) * WIN, ls] = jnp.where(low_win, both[:WIN], both[WIN:])

    for p in range(pairs):
        for block in range(2):
            intra(p, block)

    for c in range(chunks):
        exchange[c].wait_recv()

        @pl.when(pair == 0)
        def _(c=c):
            z_out[c] = (local[c] + y_in[c].astype(F32)).astype(wire)
            z_in[c] = jnp.zeros_like(z_in[c])

            @pl.when(pair < last_pair)
            def _():
                chain[c].start()

    features_q()
    for p in range(pairs):
        for block in range(1, rows // WIN):
            window(p, block)

    @pl.when(s > 0)
    def _():
        halo.wait_recv()

    @pl.when(s == 0)
    def _():
        halo_in[...] = jnp.zeros_like(halo_in)

    for p in range(pairs):
        window(p, 0)

    mine = jnp.where(inner == 1, 1.0, 0.0).astype(F32)
    total = None
    for c in range(chunks):
        lanes = slice(c * CHUNK, (c + 1) * CHUNK)

        @pl.when(pair > 0)
        def _(c=c):
            chain[c].wait_recv()

            @pl.when(pair < last_pair)
            def _():
                z_out[c] = (z_in[c].astype(F32) + (local[c] + y_in[c].astype(F32))).astype(wire)
                chain[c].start()

        earlier = z_in[c].astype(F32) + mine * y_in[c].astype(F32)
        big = jnp.concatenate(
            [
                jnp.where(mask_v[head : head + 1, lanes] > 0, earlier, 0.0).astype(BF16)
                for head in range(heads)
            ],
            axis=0,
        )
        product = dot_t(phi_q[:, lanes], big)
        if c == 0:
            lin[...] += product
        else:
            lin[...] += product

    ones = jnp.where(
        lax.broadcasted_iota(jnp.int32, (2 * LANES, LANES), 0) % LANES // HV
        == lax.broadcasted_iota(jnp.int32, (2 * LANES, LANES), 1) // HV,
        1.0,
        0.0,
    ).astype(BF16)
    for p in range(pairs):
        ls = slice(p * LANES, (p + 1) * LANES)
        linear = lin[:, ls]
        high, low = split(linear * linear)
        mean = dot(jnp.concatenate([high, low], axis=1), ones) * (1.0 / HV)
        normed = linear * lax.rsqrt(mean + 1e-05) * gain_v[:, ls]
        out[:, ls] = (normed + win[:, ls]).astype(BF16)

    for move in moves.values():
        move.wait_send()
    for move in exchange:
        move.wait_send()

    @pl.when(s < blocks - 1)
    def _():
        halo.wait_send()

    @pl.when(pair < last_pair)
    def _():
        for move in chain:
            move.wait_send()


def solution(mesh):
    blocks, group = mesh.shape["seq"], mesh.shape["head"]

    def body(hidden_states, feature_q, feature_k, value_w, window_q, window_k, norm_gain):
        rows, depth = hidden_states.shape
        heads = feature_q.shape[1] // FK
        full, width = value_w.shape
        ea, eb, mask = features(heads)
        feats = ea.shape[1]
        chunks = feats // CHUNK
        wire = BF16 if blocks <= 16 else F32
        dma, anywhere = pltpu.SemaphoreType.DMA, pl.BlockSpec(memory_space=pl.ANY)
        state = (chunks, HV, CHUNK)
        return pl.pallas_call(
            functools.partial(kernel, blocks, group, heads, wire),
            out_shape=jax.ShapeDtypeStruct((rows, width), BF16),
            in_specs=[anywhere] * 10,
            out_specs=pl.BlockSpec(memory_space=pltpu.VMEM),
            scratch_shapes=[
                pltpu.VMEM((group, rows, depth), BF16),
                pltpu.VMEM((heads * FK, full), BF16),
                pltpu.VMEM((heads * FK, full), BF16),
                pltpu.VMEM((full, width), BF16),
                pltpu.VMEM((full, width), BF16),
                pltpu.VMEM((full, width), BF16),
                pltpu.VMEM((1, width), F32),
                pltpu.VMEM(ea.shape, BF16),
                pltpu.VMEM(eb.shape, BF16),
                pltpu.VMEM(mask.shape, F32),
                pltpu.VMEM((rows, LANES), F32),
                pltpu.VMEM((rows, LANES), F32),
                pltpu.VMEM((rows, width), F32),
                pltpu.VMEM((rows, width), F32),
                pltpu.VMEM((rows, width), F32),
                pltpu.VMEM((rows, width), BF16),
                pltpu.VMEM((rows, width), BF16),
                pltpu.VMEM((rows, width), BF16),
                pltpu.VMEM((WIN, 2 * width), BF16),
                pltpu.VMEM((WIN, 2 * width), BF16),
                pltpu.VMEM((rows, feats), BF16),
                pltpu.VMEM(state, F32),
                pltpu.VMEM(state, wire),
                pltpu.VMEM(state, wire),
                pltpu.VMEM(state, wire),
                pltpu.VMEM(state, wire),
                pltpu.VMEM((rows, width), F32),
                pltpu.VMEM((rows, width), F32),
                dma((10,)),
                dma((group - 1,)),
                dma((group - 1,)),
                dma,
                dma,
                dma((chunks,)),
                dma((chunks,)),
                dma((chunks,)),
                dma((chunks,)),
            ],
            compiler_params=pltpu.CompilerParams(
                collective_id=0, has_side_effects=True, vmem_limit_bytes=66_000_000
            ),
            name="based_layer",
        )(
            hidden_states, feature_q.T, feature_k.T, value_w, window_q, window_k,
            norm_gain.reshape(1, width), jnp.asarray(ea, BF16), jnp.asarray(eb, BF16),
            jnp.asarray(mask, F32),
        )

    return jax.shard_map(
        body,
        mesh=mesh,
        in_specs=(P("seq", "head"),) + (P(None, "head"),) * 5 + (P("head"),),
        out_specs=P("seq", "head"),
        check_vma=False,
    )
```

time: 102 us -> 31.9 us (0.31)
  the two profiles are of different devices: /device:TPU:0 before, /device:TPU:24 now
where the time goes in v1:
time: 31.9 us; the launch traced here: 31.7 us
  Pallas kernels  28.8 us (90%)
  local copies, waits for them, and re-layouts  2.87 us (9%)
    pallas_call x1, Pallas kernels, body(): pl.pallas_call(functools.partial(kernel, blocks, group, heads, wire), out...  28.8 us
    unnamed x1, local copies, waits for them, and re-layouts  1.62 us
    reshape x1, local copies, waits for them, and re-layouts, body(): norm_gain.reshape(1, width)  1.24 us

profile of v1, /device:TPU:24, one launch (start us, length us, event | category | flops | bytes accessed | tf_op | source)
XLA Modules:
  0.0 31.7 jit_solution(1928933870875559266)
XLA Ops:
  0.0 1.2 %reshape.3.gain = f32[1,384]{1,0:T(1,128)} reshape(f32[384]{0:T(512)} %param.16) | data formatting | bytes 3072 | tf_op jit(solution)/shard_map/reshape | solution.py:430
  1.2 28.8 %based_layer.1 = bf16[256,384]{1,0:T(8,128)(2,1)} custom-call(bf16[256,384]{1,0:T(8,128)(2,1)} %hid.1, bf16[96,1536]{1,0:T(8,128)(2,1)} %bitcast.2, bf16[96,1536]{1,0:T(8,128)(2,1)} %bitcast.3, bf16[1536,384]{1,0:T(8,128)(2,1)} %vw.1, bf16[1536,384]{1,0:T(8,128)(2,1)} %wqw.1, bf16[1536,384]{1,0:T(8,128)(2,1)} %wkw.1, f32[1,384]{1,0:T(1,128)} %reshape.3.gain, ...), custom_call_target="tpu_custom_call" | custom-call | tf_op jit(solution)/shard_map/based_layer/pallas_call | solution.py:380
  30.1 1.6 %copy.12 = bf16[256,384]{1,0:T(8,128)(2,1)} copy(bf16[256,384]{1,0:T(8,128)(2,1)} %based_layer.1) | data formatting | bytes 393216

commit v2 on v1

--- a/solution.py
+++ b/solution.py
@@ -12,7 +12,8 @@
 HV = 64
 WIN = 64
 LANES = 128
-CHUNK = 256
+CHUNK = 128
+WIDE = 256
 MESH = pl.DeviceIdType.MESH
 F32 = jnp.float32
 BF16 = jnp.bfloat16
@@ -29,7 +30,7 @@
         owner += [head] * (1 + FK + len(upper))
         weight += [1.0] * (1 + FK) + [0.5 if i == j else 1.0 for i, j in zip(upper, lower)]
     count = len(left)
-    width = -(-count // CHUNK) * CHUNK
+    width = -(-count // WIDE) * WIDE
     ea = np.zeros((2 * LANES, width), np.float32)
     eb = np.zeros((2 * LANES, width), np.float32)
     mask = np.zeros((-(-heads // 8) * 8, width), np.float32)
@@ -168,14 +169,49 @@
                 continue
             acc[:, : heads * FK] += dot_t(tile, part_t(weight, owner))
         for acc, weight in main:
-            if final and acc is wq_acc:
+            if final and acc is not v_acc:
                 continue
             product = dot(tile, part(weight, owner))
             acc[...] = product if position == 0 else acc[...] + product
     last_tile, last_owner = tile, owner
 
     v_b[...] = v_acc[...].astype(BF16)
-    wk_b[...] = wk_acc[...].astype(BF16)
+    for load in loads[6:]:
+        load.wait()
+
+    k_high, k_low = split(k_acc[...] * FK**-0.25)
+    k_cat = jnp.concatenate([k_high, k_low], axis=1)
+    v_turned = v_b[...].T
+    exchange = []
+    for wide in range(chunks * CHUNK // WIDE):
+        lanes = slice(wide * WIDE, (wide + 1) * WIDE)
+        phi_k = (dot(k_cat, ea_v[:, lanes]) * dot(k_cat, eb_v[:, lanes])).astype(BF16)
+        full = dot(v_turned, phi_k)
+        state = full[:HV] * mask_v[0:1, lanes]
+        for head in range(1, heads):
+            state += full[head * HV : (head + 1) * HV] * mask_v[head : head + 1, lanes]
+        for piece in range(WIDE // CHUNK):
+            c = wide * (WIDE // CHUNK) + piece
+            part_state = state[:, piece * CHUNK : (piece + 1) * CHUNK]
+            local[c] = part_state
+            y_out[c] = part_state.astype(wire)
+            move = pltpu.make_async_remote_copy(
+                src_ref=y_out.at[c], dst_ref=y_in.at[c],
+                send_sem=y_send.at[c], recv_sem=y_recv.at[c],
+                device_id=(flip(s, 1), h), device_id_type=MESH,
+            )
+            move.start()
+            exchange.append(move)
+    beyond = lax.rem(s + 2, blocks)
+    chain = [
+        pltpu.make_async_remote_copy(
+            src_ref=z_out.at[c], dst_ref=z_in.at[c], send_sem=z_send.at[c], recv_sem=z_recv.at[c],
+            device_id=(beyond, h), device_id_type=MESH,
+        )
+        for c in range(chunks)
+    ]
+
+    wk_b[...] = (wk_acc[...] + dot(last_tile, part(wk_v, last_owner))).astype(BF16)
     width = heads * HV
     halo_out[:, :width] = wk_b[rows - WIN :, :]
     halo_out[:, width:] = v_b[rows - WIN :, :]
@@ -185,40 +221,11 @@
         device_id=(after, h), device_id_type=MESH,
     )
 
-    @pl.when(s < blocks - 1)
+    late = jnp.logical_and(pair == 0, inner == 1)
+
+    @pl.when(jnp.logical_and(s < blocks - 1, jnp.logical_not(late)))
     def _():
         halo.start()
-
-    for load in loads[6:]:
-        load.wait()
-
-    k_high, k_low = split(k_acc[...] * FK**-0.25)
-    k_cat = jnp.concatenate([k_high, k_low], axis=1)
-    v_turned = v_b[...].T
-    exchange = []
-    for c in range(chunks):
-        lanes = slice(c * CHUNK, (c + 1) * CHUNK)
-        phi_k = (dot(k_cat, ea_v[:, lanes]) * dot(k_cat, eb_v[:, lanes])).astype(BF16)
-        full = dot(v_turned, phi_k)
-        state = full[:HV] * mask_v[0:1, lanes]
-        for head in range(1, heads):
-            state += full[head * HV : (head + 1) * HV] * mask_v[head : head + 1, lanes]
-        local[c] = state
-        y_out[c] = state.astype(wire)
-        move = pltpu.make_async_remote_copy(
-            src_ref=y_out.at[c], dst_ref=y_in.at[c], send_sem=y_send.at[c], recv_sem=y_recv.at[c],
-            device_id=(flip(s, 1), h), device_id_type=MESH,
-        )
-        move.start()
-        exchange.append(move)
-    beyond = lax.rem(s + 2, blocks)
-    chain = [
-        pltpu.make_async_remote_copy(
-            src_ref=z_out.at[c], dst_ref=z_in.at[c], send_sem=z_send.at[c], recv_sem=z_recv.at[c],
-            device_id=(beyond, h), device_id_type=MESH,
-        )
-        for c in range(chunks)
-    ]
 
     q_acc[:, : heads * FK] += dot_t(last_tile, part_t(fq_v, last_owner))
     wq_b[...] = (wq_acc[...] + dot(last_tile, part(wq_v, last_owner))).astype(BF16)
@@ -226,8 +233,8 @@
     q_cat = jnp.concatenate([q_high, q_low], axis=1)
 
     def features_q():
-        for c in range(chunks):
-            lanes = slice(c * CHUNK, (c + 1) * CHUNK)
+        for wide in range(chunks * CHUNK // WIDE):
+            lanes = slice(wide * WIDE, (wide + 1) * WIDE)
             phi_q[:, lanes] = (dot(q_cat, ea_v[:, lanes]) * dot(q_cat, eb_v[:, lanes])).astype(BF16)
 
     k_twice = jnp.concatenate([k_high, k_high], axis=1)
@@ -291,6 +298,23 @@
             def _():
                 chain[c].start()
 
+    @pl.when(jnp.logical_and(s < blocks - 1, late))
+    def _():
+        halo.start()
+
+    def relay(c):
+        chain[c].wait_recv()
+
+        @pl.when(pair < last_pair)
+        def _():
+            z_out[c] = (z_in[c].astype(F32) + (local[c] + y_in[c].astype(F32))).astype(wire)
+            chain[c].start()
+
+    @pl.when(pair == 1)
+    def _():
+        for c in range(chunks):
+            relay(c)
+
     features_q()
     for p in range(pairs):
         for block in range(1, rows // WIN):
@@ -308,20 +332,18 @@
         window(p, 0)
 
     mine = jnp.where(inner == 1, 1.0, 0.0).astype(F32)
-    total = None
-    for c in range(chunks):
-        lanes = slice(c * CHUNK, (c + 1) * CHUNK)
-
-        @pl.when(pair > 0)
-        def _(c=c):
-            chain[c].wait_recv()
-
-            @pl.when(pair < last_pair)
-            def _():
-                z_out[c] = (z_in[c].astype(F32) + (local[c] + y_in[c].astype(F32))).astype(wire)
-                chain[c].start()
-
-        earlier = z_in[c].astype(F32) + mine * y_in[c].astype(F32)
+    for wide in range(chunks * CHUNK // WIDE):
+        lanes = slice(wide * WIDE, (wide + 1) * WIDE)
+        pieces = range(wide * (WIDE // CHUNK), (wide + 1) * (WIDE // CHUNK))
+
+        @pl.when(pair > 1)
+        def _(pieces=pieces):
+            for c in pieces:
+                relay(c)
+
+        earlier = jnp.concatenate(
+            [z_in[c].astype(F32) + mine * y_in[c].astype(F32) for c in pieces], axis=1
+        )
         big = jnp.concatenate(
             [
                 jnp.where(mask_v[head : head + 1, lanes] > 0, earlier, 0.0).astype(BF16)
@@ -329,11 +351,7 @@
             ],
             axis=0,
         )
-        product = dot_t(phi_q[:, lanes], big)
-        if c == 0:
-            lin[...] += product
-        else:
-            lin[...] += product
+        lin[...] += dot_t(phi_q[:, lanes], big)
 
     ones = jnp.where(
         lax.broadcasted_iota(jnp.int32, (2 * LANES, LANES), 0) % LANES // HV
@@ -346,7 +364,7 @@
         linear = lin[:, ls]
         high, low = split(linear * linear)
         mean = dot(jnp.concatenate([high, low], axis=1), ones) * (1.0 / HV)
-        normed = linear * lax.rsqrt(mean + 1e-05) * gain_v[:, ls]
+        normed = linear * lax.rsqrt(mean + 1e-05) * gain_v[ls].reshape(1, LANES)
         out[:, ls] = (normed + win[:, ls]).astype(BF16)
 
     for move in moves.values():
@@ -375,7 +393,7 @@
         feats = ea.shape[1]
         chunks = feats // CHUNK
         wire = BF16 if blocks <= 16 else F32
-        dma, anywhere = pltpu.SemaphoreType.DMA, pl.BlockSpec(memory_space=pl.ANY)
+        dma, anywhere = pltpu.SemaphoreType.DMA, pl.BlockSpec(memory_space=pltpu.HBM)
         state = (chunks, HV, CHUNK)
         return pl.pallas_call(
             functools.partial(kernel, blocks, group, heads, wire),
@@ -389,7 +407,7 @@
                 pltpu.VMEM((full, width), BF16),
                 pltpu.VMEM((full, width), BF16),
                 pltpu.VMEM((full, width), BF16),
-                pltpu.VMEM((1, width), F32),
+                pltpu.VMEM((width,), F32),
                 pltpu.VMEM(ea.shape, BF16),
                 pltpu.VMEM(eb.shape, BF16),
                 pltpu.VMEM(mask.shape, F32),
@@ -422,14 +440,14 @@
                 dma((chunks,)),
             ],
             compiler_params=pltpu.CompilerParams(
-                collective_id=0, has_side_effects=True, vmem_limit_bytes=66_000_000
+                collective_id=0, has_side_effects=True, vmem_limit_bytes=40 * 1024 * 1024
             ),
             name="based_layer",
-        )(
+        )(*(pltpu.with_memory_space_constraint(operand, pltpu.HBM) for operand in (
             hidden_states, feature_q.T, feature_k.T, value_w, window_q, window_k,
-            norm_gain.reshape(1, width), jnp.asarray(ea, BF16), jnp.asarray(eb, BF16),
+            norm_gain, jnp.asarray(ea, BF16), jnp.asarray(eb, BF16),
             jnp.asarray(mask, F32),
-        )
+        )))
 
     return jax.shard_map(
         body,

time: 31.9 us -> 27.2 us (0.85)
  Pallas kernels: 28.8 us -> 26.4 us
  local copies, waits for them, and re-layouts: 2.87 us -> 0.68 us
    pallas_call x1, Pallas kernels: 28.8 us -> 26.4 us  [body(): pl.pallas_call(functools.partial(kernel, blocks, group, heads, wire), out...]
    reshape x1 -> x0, local copies, waits for them, and re-layouts: 1.24 us -> none  [body(): norm_gain.reshape(1, width)]
    unnamed x1, local copies, waits for them, and re-layouts: 1.62 us -> 0.68 us
where the time goes in v2:
time: 27.2 us; the launch traced here: 27.1 us
  Pallas kernels  26.4 us (97%)
  local copies, waits for them, and re-layouts  0.68 us (2%)
    pallas_call x1, Pallas kernels, body(): pl.pallas_call(functools.partial(kernel, blocks, group, heads, wire), out...  26.4 us
    unnamed x1, local copies, waits for them, and re-layouts  0.68 us

profile of v2, /device:TPU:24, one launch (start us, length us, event | category | flops | bytes accessed | tf_op | source)
XLA Modules:
  0.0 27.1 jit_solution(3586353385722661728)
XLA Ops:
  0.0 26.4 %based_layer.1 = bf16[256,384]{1,0:T(8,128)(2,1)S(1)} custom-call(bf16[256,384]{1,0:T(8,128)(2,1)} %hid.1, bf16[96,1536]{1,0:T(8,128)(2,1)} %bitcast.2, bf16[96,1536]{1,0:T(8,128)(2,1)} %bitcast.3, bf16[1536,384]{1,0:T(8,128)(2,1)} %vw.1, bf16[1536,384]{1,0:T(8,128)(2,1)} %wqw.1, bf16[1536,384]{1,0:T(8,128)(2,1)} %wkw.1, f32[384]{0:T(512)} %gain.1, ...), custom_call_target="tpu_custom_call" | custom-call | tf_op jit(solution)/shard_map/based_layer/pallas_call | solution.py:398
  26.4 0.7 %copy.12 = bf16[256,384]{1,0:T(8,128)(2,1)} copy(bf16[256,384]{1,0:T(8,128)(2,1)S(1)} %based_layer.1) | data formatting | bytes 393216

commit v3 on v2

--- a/solution.py
+++ b/solution.py
@@ -39,6 +39,13 @@
         eb[[right[lane], LANES + right[lane]], lane] = 1.0
         mask[owner[lane], lane] = weight[lane]
     return ea, eb, mask
+
+
+def pair_range(wide, heads):
+    each = 1 + FK + FK * (FK + 1) // 2
+    first = min(wide * WIDE // each, heads - 1)
+    last = min(((wide + 1) * WIDE - 1) // each, heads - 1)
+    return first // 2, last // 2 + 1
 
 
 def dot(a, b):
@@ -186,10 +193,12 @@
     for wide in range(chunks * CHUNK // WIDE):
         lanes = slice(wide * WIDE, (wide + 1) * WIDE)
         phi_k = (dot(k_cat, ea_v[:, lanes]) * dot(k_cat, eb_v[:, lanes])).astype(BF16)
-        full = dot(v_turned, phi_k)
-        state = full[:HV] * mask_v[0:1, lanes]
-        for head in range(1, heads):
-            state += full[head * HV : (head + 1) * HV] * mask_v[head : head + 1, lanes]
+        p0, p1 = pair_range(wide, heads)
+        full = dot(v_turned[p0 * LANES : p1 * LANES], phi_k)
+        state = 0.0
+        for head in range(2 * p0, 2 * p1):
+            at = (head - 2 * p0) * HV
+            state += full[at : at + HV] * mask_v[head : head + 1, lanes]
         for piece in range(WIDE // CHUNK):
             c = wide * (WIDE // CHUNK) + piece
             part_state = state[:, piece * CHUNK : (piece + 1) * CHUNK]
@@ -227,36 +236,7 @@
     def _():
         halo.start()
 
-    q_acc[:, : heads * FK] += dot_t(last_tile, part_t(fq_v, last_owner))
     wq_b[...] = (wq_acc[...] + dot(last_tile, part(wq_v, last_owner))).astype(BF16)
-    q_high, q_low = split(q_acc[...] * FK**-0.25)
-    q_cat = jnp.concatenate([q_high, q_low], axis=1)
-
-    def features_q():
-        for wide in range(chunks * CHUNK // WIDE):
-            lanes = slice(wide * WIDE, (wide + 1) * WIDE)
-            phi_q[:, lanes] = (dot(q_cat, ea_v[:, lanes]) * dot(q_cat, eb_v[:, lanes])).astype(BF16)
-
-    k_twice = jnp.concatenate([k_high, k_high], axis=1)
-    half = rows // 2
-    lane_q = lax.broadcasted_iota(jnp.int32, (half, 2 * LANES), 1) % LANES // FK
-    low_half = lax.broadcasted_iota(jnp.int32, (half, LANES), 1) < HV
-
-    def intra(p, block):
-        rs = slice(block * half, (block + 1) * half)
-        keys = (block + 1) * half
-        qs = q_cat[rs]
-        stacked = jnp.concatenate(
-            [jnp.where(lane_q == 2 * p, qs, 0), jnp.where(lane_q == 2 * p + 1, qs, 0)], axis=0
-        )
-        a = dot_t(stacked, k_twice[:keys]) + dot_t(stacked[:, :LANES], k_low[:keys])
-        kern = 1.0 + a + 0.5 * a * a
-        row = lax.broadcasted_iota(jnp.int32, a.shape, 0) % half + block * half
-        col = lax.broadcasted_iota(jnp.int32, a.shape, 1)
-        kern = jnp.where(row >= col, kern, 0.0).astype(BF16)
-        both = dot(kern, v_b[:keys, p * LANES : (p + 1) * LANES])
-        lin[rs, p * LANES : (p + 1) * LANES] = jnp.where(low_half, both[:half], both[half:])
-
     low_win = lax.broadcasted_iota(jnp.int32, (WIN, LANES), 1) < HV
     row_w = lax.broadcasted_iota(jnp.int32, (2 * WIN, 2 * WIN), 0) % WIN
     col_w = lax.broadcasted_iota(jnp.int32, (2 * WIN, 2 * WIN), 1)
@@ -282,9 +262,12 @@
         both = dot(weights, vals)
         win[block * WIN : (block + 1) * WIN, ls] = jnp.where(low_win, both[:WIN], both[WIN:])
 
-    for p in range(pairs):
-        for block in range(2):
-            intra(p, block)
+    def windows():
+        for p in range(pairs):
+            for block in range(1, rows // WIN):
+                window(p, block)
+
+    pl.when(pair > 0)(windows)
 
     for c in range(chunks):
         exchange[c].wait_recv()
@@ -315,10 +298,40 @@
         for c in range(chunks):
             relay(c)
 
+    pl.when(pair == 0)(windows)
+    q_acc[:, : heads * FK] += dot_t(last_tile, part_t(fq_v, last_owner))
+    q_high, q_low = split(q_acc[...] * FK**-0.25)
+    q_cat = jnp.concatenate([q_high, q_low], axis=1)
+
+    def features_q():
+        for wide in range(chunks * CHUNK // WIDE):
+            lanes = slice(wide * WIDE, (wide + 1) * WIDE)
+            phi_q[:, lanes] = (dot(q_cat, ea_v[:, lanes]) * dot(q_cat, eb_v[:, lanes])).astype(BF16)
+
+    k_twice = jnp.concatenate([k_high, k_high], axis=1)
+    half = rows // 2
+    lane_q = lax.broadcasted_iota(jnp.int32, (half, 2 * LANES), 1) % LANES // FK
+    low_half = lax.broadcasted_iota(jnp.int32, (half, LANES), 1) < HV
+
+    def intra(p, block):
+        rs = slice(block * half, (block + 1) * half)
+        keys = (block + 1) * half
+        qs = q_cat[rs]
+        stacked = jnp.concatenate(
+            [jnp.where(lane_q == 2 * p, qs, 0), jnp.where(lane_q == 2 * p + 1, qs, 0)], axis=0
+        )
+        a = dot_t(stacked, k_twice[:keys]) + dot_t(stacked[:, :LANES], k_low[:keys])
+        kern = 1.0 + a + 0.5 * a * a
+        row = lax.broadcasted_iota(jnp.int32, a.shape, 0) % half + block * half
+        col = lax.broadcasted_iota(jnp.int32, a.shape, 1)
+        kern = jnp.where(row >= col, kern, 0.0).astype(BF16)
+        both = dot(kern, v_b[:keys, p * LANES : (p + 1) * LANES])
+        lin[rs, p * LANES : (p + 1) * LANES] = jnp.where(low_half, both[:half], both[half:])
+
     features_q()
     for p in range(pairs):
-        for block in range(1, rows // WIN):
-            window(p, block)
+        for block in range(2):
+            intra(p, block)
 
     @pl.when(s > 0)
     def _():
@@ -332,7 +345,24 @@
         window(p, 0)
 
     mine = jnp.where(inner == 1, 1.0, 0.0).astype(F32)
-    for wide in range(chunks * CHUNK // WIDE):
+    ones = jnp.where(
+        lax.broadcasted_iota(jnp.int32, (2 * LANES, LANES), 0) % LANES // HV
+        == lax.broadcasted_iota(jnp.int32, (2 * LANES, LANES), 1) // HV,
+        1.0,
+        0.0,
+    ).astype(BF16)
+
+    def finish(p):
+        ls = slice(p * LANES, (p + 1) * LANES)
+        linear = lin[:, ls]
+        high, low = split(linear * linear)
+        mean = dot(jnp.concatenate([high, low], axis=1), ones) * (1.0 / HV)
+        normed = linear * lax.rsqrt(mean + 1e-05) * gain_v[ls].reshape(1, LANES)
+        out[:, ls] = (normed + win[:, ls]).astype(BF16)
+
+    finished = 0
+    wides = chunks * CHUNK // WIDE
+    for wide in range(wides):
         lanes = slice(wide * WIDE, (wide + 1) * WIDE)
         pieces = range(wide * (WIDE // CHUNK), (wide + 1) * (WIDE // CHUNK))
 
@@ -341,31 +371,22 @@
             for c in pieces:
                 relay(c)
 
+        p0, p1 = pair_range(wide, heads)
         earlier = jnp.concatenate(
             [z_in[c].astype(F32) + mine * y_in[c].astype(F32) for c in pieces], axis=1
         )
         big = jnp.concatenate(
             [
                 jnp.where(mask_v[head : head + 1, lanes] > 0, earlier, 0.0).astype(BF16)
-                for head in range(heads)
+                for head in range(2 * p0, 2 * p1)
             ],
             axis=0,
         )
-        lin[...] += dot_t(phi_q[:, lanes], big)
-
-    ones = jnp.where(
-        lax.broadcasted_iota(jnp.int32, (2 * LANES, LANES), 0) % LANES // HV
-        == lax.broadcasted_iota(jnp.int32, (2 * LANES, LANES), 1) // HV,
-        1.0,
-        0.0,
-    ).astype(BF16)
-    for p in range(pairs):
-        ls = slice(p * LANES, (p + 1) * LANES)
-        linear = lin[:, ls]
-        high, low = split(linear * linear)
-        mean = dot(jnp.concatenate([high, low], axis=1), ones) * (1.0 / HV)
-        normed = linear * lax.rsqrt(mean + 1e-05) * gain_v[ls].reshape(1, LANES)
-        out[:, ls] = (normed + win[:, ls]).astype(BF16)
+        lin[:, p0 * LANES : p1 * LANES] += dot_t(phi_q[:, lanes], big)
+        ready = pairs if wide + 1 == wides else pair_range(wide + 1, heads)[0]
+        for p in range(finished, ready):
+            finish(p)
+        finished = max(finished, ready)
 
     for move in moves.values():
         move.wait_send()

time: 27.2 us -> 25.8 us (0.949)
  Pallas kernels: 26.4 us -> 25 us
    pallas_call x1, Pallas kernels: 26.4 us -> 25 us  [body(): pl.pallas_call(functools.partial(kernel, blocks, group, heads, wire), out...]
where the time goes in v3:
time: 25.8 us; the launch traced here: 25.6 us
  Pallas kernels  25 us (97%)
  local copies, waits for them, and re-layouts  0.68 us (3%)
    pallas_call x1, Pallas kernels, body(): pl.pallas_call(functools.partial(kernel, blocks, group, heads, wire), out...  25 us
    unnamed x1, local copies, waits for them, and re-layouts  0.68 us

profile of v3, /device:TPU:24, one launch (start us, length us, event | category | flops | bytes accessed | tf_op | source)
XLA Modules:
  0.0 25.6 jit_solution(9685273171539983518)
XLA Ops:
  0.0 25.0 %based_layer.1 = bf16[256,384]{1,0:T(8,128)(2,1)S(1)} custom-call(bf16[256,384]{1,0:T(8,128)(2,1)} %hid.1, bf16[96,1536]{1,0:T(8,128)(2,1)} %bitcast.2, bf16[96,1536]{1,0:T(8,128)(2,1)} %bitcast.3, bf16[1536,384]{1,0:T(8,128)(2,1)} %vw.1, bf16[1536,384]{1,0:T(8,128)(2,1)} %wqw.1, bf16[1536,384]{1,0:T(8,128)(2,1)} %wkw.1, f32[384]{0:T(512)} %gain.1, ...), custom_call_target="tpu_custom_call" | custom-call | tf_op jit(solution)/shard_map/based_layer/pallas_call | solution.py:419
  25.0 0.7 %copy.12 = bf16[256,384]{1,0:T(8,128)(2,1)} copy(bf16[256,384]{1,0:T(8,128)(2,1)S(1)} %based_layer.1) | data formatting | bytes 393216

commit v4 on v3

--- a/solution.py
+++ b/solution.py
@@ -183,6 +183,26 @@
     last_tile, last_owner = tile, owner
 
     v_b[...] = v_acc[...].astype(BF16)
+    width = heads * HV
+    after = lax.rem(s + 1, blocks)
+    halo = pltpu.make_async_remote_copy(
+        src_ref=halo_out, dst_ref=halo_in, send_sem=h_send, recv_sem=h_recv,
+        device_id=(after, h), device_id_type=MESH,
+    )
+
+    def window_keys():
+        wk_b[...] = (wk_acc[...] + dot(last_tile, part(wk_v, last_owner))).astype(BF16)
+        halo_out[:, :width] = wk_b[rows - WIN :, :]
+        halo_out[:, width:] = v_b[rows - WIN :, :]
+
+    @pl.when(pair > 0)
+    def _():
+        window_keys()
+
+        @pl.when(s < blocks - 1)
+        def _():
+            halo.start()
+
     for load in loads[6:]:
         load.wait()
 
@@ -220,21 +240,13 @@
         for c in range(chunks)
     ]
 
-    wk_b[...] = (wk_acc[...] + dot(last_tile, part(wk_v, last_owner))).astype(BF16)
-    width = heads * HV
-    halo_out[:, :width] = wk_b[rows - WIN :, :]
-    halo_out[:, width:] = v_b[rows - WIN :, :]
-    after = lax.rem(s + 1, blocks)
-    halo = pltpu.make_async_remote_copy(
-        src_ref=halo_out, dst_ref=halo_in, send_sem=h_send, recv_sem=h_recv,
-        device_id=(after, h), device_id_type=MESH,
-    )
-
-    late = jnp.logical_and(pair == 0, inner == 1)
-
-    @pl.when(jnp.logical_and(s < blocks - 1, jnp.logical_not(late)))
-    def _():
-        halo.start()
+    @pl.when(pair == 0)
+    def _():
+        window_keys()
+
+        @pl.when(jnp.logical_and(s < blocks - 1, inner == 0))
+        def _():
+            halo.start()
 
     wq_b[...] = (wq_acc[...] + dot(last_tile, part(wq_v, last_owner))).astype(BF16)
     low_win = lax.broadcasted_iota(jnp.int32, (WIN, LANES), 1) < HV
@@ -262,30 +274,45 @@
         both = dot(weights, vals)
         win[block * WIN : (block + 1) * WIN, ls] = jnp.where(low_win, both[:WIN], both[WIN:])
 
-    def windows():
+    spots = [(p, block) for p in range(pairs) for block in range(1, rows // WIN)]
+
+    def rest():
+        q_acc[:, : heads * FK] += dot_t(last_tile, part_t(fq_v, last_owner))
+        q_high, q_low = split(q_acc[...] * FK**-0.25)
+        q_cat = jnp.concatenate([q_high, q_low], axis=1)
+
+        def features_q():
+            for wide in range(chunks * CHUNK // WIDE):
+                lanes = slice(wide * WIDE, (wide + 1) * WIDE)
+                phi_q[:, lanes] = (dot(q_cat, ea_v[:, lanes]) * dot(q_cat, eb_v[:, lanes])).astype(BF16)
+
+        k_twice = jnp.concatenate([k_high, k_high], axis=1)
+        half = rows // 2
+        lane_q = lax.broadcasted_iota(jnp.int32, (half, 2 * LANES), 1) % LANES // FK
+        low_half = lax.broadcasted_iota(jnp.int32, (half, LANES), 1) < HV
+
+        def intra(p, block):
+            rs = slice(block * half, (block + 1) * half)
+            keys = (block + 1) * half
+            qs = q_cat[rs]
+            stacked = jnp.concatenate(
+                [jnp.where(lane_q == 2 * p, qs, 0), jnp.where(lane_q == 2 * p + 1, qs, 0)], axis=0
+            )
+            a = dot_t(stacked, k_twice[:keys]) + dot_t(stacked[:, :LANES], k_low[:keys])
+            kern = 1.0 + a + 0.5 * a * a
+            row = lax.broadcasted_iota(jnp.int32, a.shape, 0) % half + block * half
+            col = lax.broadcasted_iota(jnp.int32, a.shape, 1)
+            kern = jnp.where(row >= col, kern, 0.0).astype(BF16)
+            both = dot(kern, v_b[:keys, p * LANES : (p + 1) * LANES])
+            lin[rs, p * LANES : (p + 1) * LANES] = jnp.where(low_half, both[:half], both[half:])
+
+        features_q()
         for p in range(pairs):
-            for block in range(1, rows // WIN):
-                window(p, block)
-
-    pl.when(pair > 0)(windows)
-
-    for c in range(chunks):
+            for block in range(2):
+                intra(p, block)
+
+    def relay(c):
         exchange[c].wait_recv()
-
-        @pl.when(pair == 0)
-        def _(c=c):
-            z_out[c] = (local[c] + y_in[c].astype(F32)).astype(wire)
-            z_in[c] = jnp.zeros_like(z_in[c])
-
-            @pl.when(pair < last_pair)
-            def _():
-                chain[c].start()
-
-    @pl.when(jnp.logical_and(s < blocks - 1, late))
-    def _():
-        halo.start()
-
-    def relay(c):
         chain[c].wait_recv()
 
         @pl.when(pair < last_pair)
@@ -293,45 +320,41 @@
             z_out[c] = (z_in[c].astype(F32) + (local[c] + y_in[c].astype(F32))).astype(wire)
             chain[c].start()
 
+    @pl.when(pair == 0)
+    def _():
+        for c in range(chunks):
+            exchange[c].wait_recv()
+            z_out[c] = (local[c] + y_in[c].astype(F32)).astype(wire)
+            z_in[c] = jnp.zeros_like(z_in[c])
+
+            @pl.when(pair < last_pair)
+            def _(c=c):
+                chain[c].start()
+
+            for spot in spots[c :: chunks]:
+                window(*spot)
+
+        @pl.when(jnp.logical_and(s < blocks - 1, inner == 1))
+        def _():
+            halo.start()
+
+    pl.when(pair > 0)(rest)
+
+    @pl.when(pair > 1)
+    def _():
+        for spot in spots:
+            window(*spot)
+
     @pl.when(pair == 1)
     def _():
+        for spot in spots[:2]:
+            window(*spot)
         for c in range(chunks):
             relay(c)
-
-    pl.when(pair == 0)(windows)
-    q_acc[:, : heads * FK] += dot_t(last_tile, part_t(fq_v, last_owner))
-    q_high, q_low = split(q_acc[...] * FK**-0.25)
-    q_cat = jnp.concatenate([q_high, q_low], axis=1)
-
-    def features_q():
-        for wide in range(chunks * CHUNK // WIDE):
-            lanes = slice(wide * WIDE, (wide + 1) * WIDE)
-            phi_q[:, lanes] = (dot(q_cat, ea_v[:, lanes]) * dot(q_cat, eb_v[:, lanes])).astype(BF16)
-
-    k_twice = jnp.concatenate([k_high, k_high], axis=1)
-    half = rows // 2
-    lane_q = lax.broadcasted_iota(jnp.int32, (half, 2 * LANES), 1) % LANES // FK
-    low_half = lax.broadcasted_iota(jnp.int32, (half, LANES), 1) < HV
-
-    def intra(p, block):
-        rs = slice(block * half, (block + 1) * half)
-        keys = (block + 1) * half
-        qs = q_cat[rs]
-        stacked = jnp.concatenate(
-            [jnp.where(lane_q == 2 * p, qs, 0), jnp.where(lane_q == 2 * p + 1, qs, 0)], axis=0
-        )
-        a = dot_t(stacked, k_twice[:keys]) + dot_t(stacked[:, :LANES], k_low[:keys])
-        kern = 1.0 + a + 0.5 * a * a
-        row = lax.broadcasted_iota(jnp.int32, a.shape, 0) % half + block * half
-        col = lax.broadcasted_iota(jnp.int32, a.shape, 1)
-        kern = jnp.where(row >= col, kern, 0.0).astype(BF16)
-        both = dot(kern, v_b[:keys, p * LANES : (p + 1) * LANES])
-        lin[rs, p * LANES : (p + 1) * LANES] = jnp.where(low_half, both[:half], both[half:])
-
-    features_q()
-    for p in range(pairs):
-        for block in range(2):
-            intra(p, block)
+            for spot in spots[2 + c :: chunks]:
+                window(*spot)
+
+    pl.when(pair == 0)(rest)
 
     @pl.when(s > 0)
     def _():

time: 25.8 us -> 24.2 us (0.938)
  Pallas kernels: 25 us -> 23.3 us
    pallas_call x1, Pallas kernels: 25 us -> 23.3 us  [body(): pl.pallas_call(functools.partial(kernel, blocks, group, heads, wire), out...]
where the time goes in v4:
time: 24.2 us; the launch traced here: 24 us
  Pallas kernels  23.3 us (96%)
  local copies, waits for them, and re-layouts  0.68 us (3%)
    pallas_call x1, Pallas kernels, body(): pl.pallas_call(functools.partial(kernel, blocks, group, heads, wire), out...  23.3 us
    unnamed x1, local copies, waits for them, and re-layouts  0.68 us

profile of v4, /device:TPU:24, one launch (start us, length us, event | category | flops | bytes accessed | tf_op | source)
XLA Modules:
  0.0 24.0 jit_solution(12852948704492010453)
XLA Ops:
  0.0 23.3 %based_layer.1 = bf16[256,384]{1,0:T(8,128)(2,1)S(1)} custom-call(bf16[256,384]{1,0:T(8,128)(2,1)} %hid.1, bf16[96,1536]{1,0:T(8,128)(2,1)} %bitcast.2, bf16[96,1536]{1,0:T(8,128)(2,1)} %bitcast.3, bf16[1536,384]{1,0:T(8,128)(2,1)} %vw.1, bf16[1536,384]{1,0:T(8,128)(2,1)} %wqw.1, bf16[1536,384]{1,0:T(8,128)(2,1)} %wkw.1, f32[384]{0:T(512)} %gain.1, ...), custom_call_target="tpu_custom_call" | custom-call | tf_op jit(solution)/shard_map/based_layer/pallas_call | solution.py:442
  23.3 0.7 %copy.12 = bf16[256,384]{1,0:T(8,128)(2,1)} copy(bf16[256,384]{1,0:T(8,128)(2,1)S(1)} %based_layer.1) | data formatting | bytes 393216
